TPU v7x, 32 devices: a whole 2x2x4 slice. The times are simulated.
32 devices in a mesh: grp: 2 (over y), row: 4 (over x, core), col: 4 (over z).
Axes of the slice: x: 2, y: 2, z: 4, core: 2. Of those that a mesh axis runs over, the one named last changes fastest.
Arguments:
- perturbation: bfloat16 [4, 12000, 12000], P('grp', 'row', 'col'), parts along dimension 0, may hold values from -96 to 96
- occ_coeffs: bfloat16 [12000, 2000], P('row', 'col'), may hold values from -0.0546875 to 0.0546875
- vir_coeffs: bfloat16 [12000, 512], P('col', 'row'), may hold values from -0.0546875 to 0.0546875
- occ_energies: float32 [2000], replicated, may hold values from -1 to -0.1
- vir_energies: float32 [512], replicated, may hold values from 0.1 to 1.5
Outputs:
- density_response: bfloat16 [4, 12000, 12000], P('grp', 'row', 'col'), parts along dimension 0
There are 2 independent parts, one for each index of `grp`. A program takes and returns all parts, laid end to end along the dimension named above; an argument that names none is the same for every part. Nothing has to cross between parts.
All inputs are finite; a program needn't handle non-finite values.
Results may differ from a plain program's by a relative error of at most 0.0098.
Values may be sent and summed in bfloat16 or wider, within the bound.
A program may use at most 192 MiB of HBM per device.

v0:
```python
import jax
import jax.numpy as jnp
from jax import lax
from jax.sharding import PartitionSpec as P


def per_device(perturbation, occ_coeffs, vir_coeffs, occ_energies, vir_energies):
    occ_rows = lax.all_gather(occ_coeffs, "col", axis=1, tiled=True)
    vir_rows = lax.all_gather(vir_coeffs, "row", axis=1, tiled=True)
    image = jnp.einsum("pij,jv->piv", perturbation, vir_rows, preferred_element_type=jnp.float32)
    image = lax.psum(image, "col")
    partial_value = jnp.einsum(
        "io,piv->pov", occ_rows.astype(jnp.float32), image, precision=lax.Precision.HIGHEST
    )
    coupling = lax.psum(partial_value, "row")
    gaps = occ_energies[:, None] - vir_energies[None, :]
    response = (coupling / gaps[None, :, :]).astype(jnp.bfloat16)
    mixed = jnp.einsum(
        "io,pov->piv", occ_rows, response, preferred_element_type=jnp.float32
    ).astype(jnp.bfloat16)
    return jnp.einsum("piv,jv->pij", mixed, vir_rows, preferred_element_type=jnp.float32).astype(
        jnp.bfloat16
    )


def solution(mesh):
    placed = (P("grp", "row", "col"), P("row", "col"), P("col", "row"), P(), P())
    return jax.shard_map(
        per_device, mesh=mesh, in_specs=placed, out_specs=P("grp", "row", "col"), check_vma=False
    )
```

profile of v0, /device:TPU:0, one launch (start us, length us, event | category | flops | bytes accessed | tf_op | source)
XLA Modules:
  0.0 920.3 jit_solution(8147711302796807755)
XLA Ops:
  6.5 0.0 all-gather.4.cloned.1.call-start
  6.5 0.7 all-gather.4.cloned.1.call-update
  7.3 0.0 all-gather.6.cloned.1.call-start
  7.3 0.7 all-gather.6.cloned.1.call-update
  8.0 0.0 all-reduce.3.cloned.1.call-start
  8.1 32.1 %all-gather.4.cloned.1.call-done = bf16[3000,512]{1,0:T(8,128)(2,1)} async-done(((bf16[3000,128]{1,0:T(8,128)(2,1)}), bf16[3000,512]{1,0:T(8,128)(2,1)}) %all-gather.4.cloned.1.call-update) | async-done | bytes 3072016 | tf_op jit(solution)/shard_map/all_gather | solution.py:9
  40.1 26.8 %fusion.6 = f32[2,3000,512]{2,1,0:T(8,128)} fusion(bf16[2,3000,3000]{2,1,0:T(8,128)(2,1)} %param.5, bf16[3000,512]{1,0:T(8,128)(2,1)} %all-gather.4.cloned.1.call-done), kind=kOutput, calls=%fused_computation.9 | convolution fusion | flops 18432000000 | bytes 51360000 | tf_op jit(solution)/shard_map/pij,jv->piv/dot_general | solution.py:10
  66.9 0.0 all-reduce.3.cloned.1.call-update
  66.9 0.0 all-reduce.5.cloned.1.call-start
  67.0 188.1 %all-gather.6.cloned.1.call-done = bf16[4,500,3000]{1,2,0:T(8,128)(2,1)} async-done(((bf16[1,500,3000]{1,2,0:T(8,128)(2,1)}), bf16[4,500,3000]{1,2,0:T(8,128)(2,1)}) %all-gather.6.cloned.1.call-update) | async-done | bytes 12000016 | tf_op jit(solution)/shard_map/all_gather | solution.py:8
  255.1 16.1 %copy.7 = bf16[4,500,3000]{2,1,0:T(8,128)(2,1)} copy(bf16[4,500,3000]{1,2,0:T(8,128)(2,1)} %all-gather.6.cloned.1.call-done) | data formatting | bytes 24000000 | tf_op jit(solution)/shard_map/all_gather | solution.py:8
  271.2 16.2 %reshape.30 = bf16[2000,3000,1]{1,0,2:T(8,128)(2,1)} reshape(bf16[4,500,3000]{2,1,0:T(8,128)(2,1)} %copy.7) | data formatting | bytes 24000000
  287.4 385.4 %all-reduce.3.cloned.1.call-done = f32[2,3000,512]{2,1,0:T(8,128)} async-done(((f32[2,3000,512]{2,1,0:T(8,128)}), f32[2,3000,512]{2,1,0:T(8,128)}) %all-reduce.3.cloned.1.call-update) | async-done | bytes 12288016 | tf_op jit(solution)/shard_map/psum | solution.py:11
  672.7 44.9 %convolution_bitcast_fusion = f32[2,2000,512]{2,1,0:T(8,128)} fusion(f32[2,3000,512]{2,1,0:T(8,128)} %all-reduce.3.cloned.1.call-done, bf16[2000,3000,1]{1,0,2:T(8,128)(2,1)} %reshape.30), kind=kOutput, calls=%fused_computation.6 | convolution fusion | flops 73728000000 | bytes 32480000 | tf_op jit(solution)/shard_map/io,piv->pov/dot_general | solution.py:12
  717.7 0.0 copy-start
  717.7 0.0 copy-start.1
  717.7 0.0 all-reduce.5.cloned.1.call-update
  717.7 0.7 copy-done
  718.4 0.0 copy-done.1
  718.4 2.3 broadcast_subtract_fusion
  720.7 17.0 %reshape.28 = bf16[2000,3000]{1,0:T(8,128)(2,1)} reshape(bf16[4,500,3000]{2,1,0:T(8,128)(2,1)} %copy.7) | data formatting | bytes 24000000
  737.7 0.0 copy-start.2
  737.7 128.8 %all-reduce.5.cloned.1.call-done = f32[2,2000,512]{2,1,0:T(8,128)} async-done(((f32[2,2000,512]{2,1,0:T(8,128)}), f32[2,2000,512]{2,1,0:T(8,128)}) %all-reduce.5.cloned.1.call-update) | async-done | bytes 8192016 | tf_op jit(solution)/shard_map/psum | solution.py:15
  866.5 20.9 %fusion = bf16[2,512,3000]{1,2,0:T(8,128)(2,1)} fusion(bf16[2000,3000]{1,0:T(8,128)(2,1)} %reshape.28, f32[2,2000,512]{2,1,0:T(8,128)} %all-reduce.5.cloned.1.call-done, f32[2000,512]{1,0:T(8,128)} %broadcast_subtract_fusion), kind=kOutput, calls=%fused_computation.1 | convolution fusion | flops 12292096000 | bytes 30432000 | tf_op jit(solution)/shard_map/io,pov->piv/dot_general | solution.py:18
  887.3 0.0 copy-done.2
  887.3 26.4 %convolution_convert_fusion = bf16[2,3000,3000]{2,1,0:T(8,128)(2,1)} fusion(bf16[2,512,3000]{1,2,0:T(8,128)(2,1)} %fusion, bf16[3000,512]{1,0:T(8,128)(2,1)S(1)} %copy-done.2), kind=kOutput, calls=%fused_computation | convolution fusion | flops 18449999872 | bytes 45216000 | tf_op jit(solution)/shard_map/piv,jv->pij/dot_general | solution.py:21
Async XLA Ops:
  6.5 33.6 %all-gather.4.cloned.1.call-start = ((), (), s32[]{:S(2)}) async-start(), calls=%async_computation | async-start | bytes 3840000 | tf_op jit(solution)/shard_map/all_gather | solution.py:9
  7.3 247.8 %all-gather.6.cloned.1.call-start = ((), (), s32[]{:S(2)}) async-start(), calls=%async_computation.3 | async-start | bytes 15360000 | tf_op jit(solution)/shard_map/all_gather | solution.py:8
  8.0 664.7 %all-reduce.3.cloned.1.call-start = ((), (), s32[]{:S(2)}) async-start(), calls=%async_computation.1 | async-start | bytes 24576000 | tf_op jit(solution)/shard_map/psum | solution.py:11
  66.9 799.5 %all-reduce.5.cloned.1.call-start = ((), (), s32[]{:S(2)}) async-start(), calls=%async_computation.2 | async-start | bytes 16384000 | tf_op jit(solution)/shard_map/psum | solution.py:15
  717.7 0.7 copy-start
  717.7 0.7 copy-start.1
  737.7 149.7 %copy-start.2 = (bf16[3000,512]{1,0:T(8,128)(2,1)S(1)}, bf16[3000,512]{1,0:T(8,128)(2,1)}, u32[]{:S(2)}) copy-start(bf16[3000,512]{1,0:T(8,128)(2,1)} %all-gather.4.cloned.1.call-done) | copy-start | bytes 9216004
Sparse Core Ops, SparseCore 0:
  8.9 31.1 all-gather.3
  41.7 213.3 all-gather.5
  257.6 415.1 all-reduce.2
  717.8 148.6 all-reduce.4
where the time goes:
time: 921 us; the launch traced here: 920 us
  waiting for transfers between devices  736 us (80%)
  matrix products  119 us (13%)
  local copies, waits for them, and re-layouts  50 us (5%)
  between operations  13.1 us (1%)
    psum x1, waiting for transfers between devices, per_device(): image = lax.psum(image, 'col')  385 us
    all_gather x1, waiting for transfers between devices, per_device(): occ_rows = lax.all_gather(occ_coeffs, 'col', axis=1, tiled=True)  188 us
    psum x1, waiting for transfers between devices, per_device(): coupling = lax.psum(partial_value, 'row')  129 us
    dot_general x1, matrix products, per_device(): jnp.einsum('io,piv->pov', occ_rows.astype(jnp.float32), image, precision=...  44.9 us
    unnamed x8, local copies, waits for them, and re-layouts  33.9 us
    all_gather x1, waiting for transfers between devices, per_device(): vir_rows = lax.all_gather(vir_coeffs, 'row', axis=1, tiled=True)  32.1 us
    dot_general x1, matrix products, per_device(): jnp.einsum('pij,jv->piv', perturbation, vir_rows, preferred_element_type=...  26.8 us
    dot_general x1, matrix products, per_device(): jnp.einsum('piv,jv->pij', mixed, vir_rows, preferred_element_type=jnp.flo...  26.4 us
  transfers between devices with their start and end apart: 4, of which 4 were waited for; matrix products, arithmetic and copies ran while one was open for 9% of the time, Pallas kernels for 0%

commit v1 on v0

v1 whole, which is shorter than its diff:
```python
import jax
import jax.numpy as jnp
from jax import lax
from jax.sharding import PartitionSpec as P

BF16 = jnp.bfloat16
F32 = jnp.float32


def per_device(perturbation, occ_coeffs, vir_coeffs, occ_energies, vir_energies):
    vir_rows = lax.all_gather(vir_coeffs, "row", axis=1, tiled=True)
    occ_parts = lax.all_gather(occ_coeffs, "col")
    cols, _, width = occ_parts.shape
    image = jnp.einsum(
        "pij,jv->piv", perturbation, vir_rows, preferred_element_type=F32
    ).astype(BF16)
    part = jnp.einsum("cio,piv->pcov", occ_parts, image, preferred_element_type=F32).astype(BF16)
    coupling = lax.psum(part, ("row", "col"))
    gaps = occ_energies.reshape(cols, width)[:, :, None] - vir_energies[None, None, :]
    response = (coupling.astype(F32) / gaps[None]).astype(BF16)
    mixed = jnp.einsum("cio,pcov->piv", occ_parts, response, preferred_element_type=F32).astype(BF16)
    return jnp.einsum("piv,jv->pij", mixed, vir_rows, preferred_element_type=F32).astype(BF16)


def solution(mesh):
    placed = (P("grp", "row", "col"), P("row", "col"), P("col", "row"), P(), P())
    return jax.shard_map(
        per_device, mesh=mesh, in_specs=placed, out_specs=P("grp", "row", "col"), check_vma=False
    )
```

time: 921 us -> 448 us (0.49)
  waiting for transfers between devices: 736 us -> 329 us
  local copies, waits for them, and re-layouts: 50 us -> 7.93 us
  matrix products: 119 us -> 89.4 us
    psum x2 -> x1, waiting for transfers between devices: 514 us -> 107 us  [per_device(): coupling = lax.psum(part, ('row', 'col'))]
    dot_general x3, matrix products: 92.2 us -> 63.5 us  [the longest x1 27.6 us: per_device(): jnp.einsum('piv,jv->pij', mixed, vir_rows, preferred_element_type=F32)]
    unnamed x8 -> x5, local copies, waits for them, and re-layouts: 33.9 us -> 7.85 us
    all_gather x1 -> x0, local copies, waits for them, and re-layouts: 16.1 us -> none  [per_device(): occ_rows = lax.all_gather(occ_coeffs, 'col', axis=1, tiled=True)]
  transfers between devices with their start and end apart: 4 -> 3, of which waited for: 4 -> 3; matrix products, arithmetic and copies ran while one was open for 9% -> 6% of each run, Pallas kernels for 0% -> 0%
where the time goes in v1:
time: 448 us
  waiting for transfers between devices  329 us (73%)
  matrix products  89.4 us (20%)
  between operations  13.1 us (3%)
  other arithmetic  8.38 us (2%)
  local copies, waits for them, and re-layouts  7.93 us (2%)
    all_gather x1, waiting for transfers between devices, per_device(): occ_parts = lax.all_gather(occ_coeffs, 'col')  189 us
    psum x1, waiting for transfers between devices, per_device(): coupling = lax.psum(part, ('row', 'col'))  107 us
    all_gather x1, waiting for transfers between devices, per_device(): vir_rows = lax.all_gather(vir_coeffs, 'row', axis=1, tiled=True)  32.1 us
    dot_general x1, matrix products, per_device(): jnp.einsum('piv,jv->pij', mixed, vir_rows, preferred_element_type=F32)  27.6 us
    dot_general x1, matrix products, per_device(): jnp.einsum('pij,jv->piv', perturbation, vir_rows, preferred_element_type=...  25.8 us
    dot_general x1, matrix products, per_device(): jnp.einsum('cio,piv->pcov', occ_parts, image, preferred_element_type=F32)  19.1 us
    dot_general x1, matrix products, per_device(): jnp.einsum('cio,pcov->piv', occ_parts, response, preferred_element_type=F32)  16.8 us
  transfers between devices with their start and end apart: 3, of which 3 were waited for; matrix products, arithmetic and copies ran while one was open for 6% of the time, Pallas kernels for 0%

profile of v1, /device:TPU:0, one launch (start us, length us, event | category | flops | bytes accessed | tf_op | source)
XLA Modules:
  0.0 448.0 jit_solution(10581064769501468559)
XLA Ops:
  6.5 0.0 all-gather.4.cloned.1.call-start
  6.5 0.7 all-gather.4.cloned.1.call-update
  7.3 0.0 all-gather.6.cloned.1.call-start
  7.3 0.7 all-gather.6.cloned.1.call-update
  8.0 0.0 all-reduce.2.cloned.1.call-start
  8.1 32.1 %all-gather.4.cloned.1.call-done = bf16[3000,512]{1,0:T(8,128)(2,1)} async-done(((bf16[3000,128]{1,0:T(8,128)(2,1)}), bf16[3000,512]{1,0:T(8,128)(2,1)}) %all-gather.4.cloned.1.call-update) | async-done | bytes 3072016 | tf_op jit(solution)/shard_map/all_gather | solution.py:11
  40.1 25.8 %fusion.45 = bf16[2,3000,512,1]{2,1,3,0:T(8,128)(2,1)} fusion(bf16[2,3000,3000]{2,1,0:T(8,128)(2,1)} %param.5, bf16[3000,512]{1,0:T(8,128)(2,1)} %all-gather.4.cloned.1.call-done), kind=kOutput, calls=%fused_computation.5.clone.clone.clone.1 | convolution fusion | flops 18435072000 | bytes 45216000 | tf_op jit(solution)/shard_map/pij,jv->piv/dot_general | solution.py:14
  66.0 189.1 %all-gather.6.cloned.1.call-done = bf16[12000,500]{1,0:T(8,128)(2,1)} async-done(((bf16[3000,500]{1,0:T(8,128)(2,1)}), bf16[12000,500]{1,0:T(8,128)(2,1)}) %all-gather.6.cloned.1.call-update) | async-done | bytes 12000016 | tf_op jit(solution)/shard_map/all_gather | solution.py:12
  255.1 19.1 %fusion.17 = bf16[2,512,4,500]{1,3,2,0:T(8,128)(2,1)} fusion(bf16[4,3000,500,1]{2,1,0,3:T(8,128)(2,1)} %bitcast.58, bf16[2,3000,512,1]{2,1,3,0:T(8,128)(2,1)} %fusion.45), kind=kOutput, calls=%fused_computation.12 | convolution fusion | flops 12290048000 | bytes 22240000 | tf_op jit(solution)/shard_map/cio,piv->pcov/dot_general | solution.py:17
  274.2 0.0 copy-start
  274.2 0.0 copy-start.1
  274.2 7.8 %copy.10 = bf16[2,512,4,500]{3,2,1,0:T(4,128)(2,1)} copy(bf16[2,512,4,500]{1,3,2,0:T(8,128)(2,1)} %fusion.17) | data formatting | bytes 8192000
  282.0 0.0 all-reduce.2.cloned.1.call-update
  282.0 0.0 copy-done
  282.1 0.1 sub.19
  282.1 0.0 copy-done.1
  282.1 2.8 broadcast_subtract_fusion
  285.0 106.6 %all-reduce.2.cloned.1.call-done = bf16[2,4,500,512]{2,1,3,0:T(4,128)(2,1)} async-done(((bf16[2,4,500,512]{2,1,3,0:T(4,128)(2,1)}), bf16[2,4,500,512]{2,1,3,0:T(4,128)(2,1)}) %all-reduce.2.cloned.1.call-update) | async-done | bytes 4096016 | tf_op jit(solution)/shard_map/psum | solution.py:18
  391.5 5.5 %fusion = bf16[2,4,500,512]{2,1,3,0:T(4,128)(2,1)S(1)} fusion(bf16[2,4,500,512]{2,1,3,0:T(4,128)(2,1)} %all-reduce.2.cloned.1.call-done, f32[4,500,512]{1,0,2:T(4,128)} %broadcast_subtract_fusion), kind=kLoop, calls=%fused_computation.3 | loop fusion | flops 6144000 | bytes 12288000 | tf_op jit(solution)/shard_map/convert_element_type | solution.py:20
  397.1 16.8 %fusion.41 = bf16[2,3000,512]{2,1,0:T(8,128)(2,1)} fusion(bf16[4,3000,500,1]{2,1,0,3:T(8,128)(2,1)} %bitcast.59, bf16[2,4,500,512]{2,1,3,0:T(4,128)(2,1)S(1)} %fusion), kind=kOutput, calls=%fused_computation.6.clone.1 | convolution fusion | flops 12291072000 | bytes 22240000 | tf_op jit(solution)/shard_map/cio,pcov->piv/dot_general | solution.py:21
  413.9 27.6 %convolution_convert_fusion = bf16[2,3000,3000]{2,1,0:T(8,128)(2,1)} fusion(bf16[3000,512]{1,0:T(8,128)(2,1)} %all-gather.4.cloned.1.call-done, bf16[2,3000,512]{2,1,0:T(8,128)(2,1)} %fusion.41), kind=kOutput, calls=%fused_computation | convolution fusion | flops 18449999872 | bytes 45216000 | tf_op jit(solution)/shard_map/piv,jv->pij/dot_general | solution.py:22
Async XLA Ops:
  6.5 33.6 %all-gather.4.cloned.1.call-start = ((), (), s32[]{:S(2)}) async-start(), calls=%async_computation | async-start | bytes 3840000 | tf_op jit(solution)/shard_map/all_gather | solution.py:11
  7.3 247.8 %all-gather.6.cloned.1.call-start = ((), (), s32[]{:S(2)}) async-start(), calls=%async_computation.2 | async-start | bytes 15360000 | tf_op jit(solution)/shard_map/all_gather | solution.py:12
  8.0 383.5 %all-reduce.2.cloned.1.call-start = ((), (), s32[]{:S(2)}) async-start(), calls=%async_computation.1 | async-start | bytes 8388608 | tf_op jit(solution)/shard_map/psum | solution.py:18
  274.2 7.9 %copy-start = (f32[2000]{0:T(1024)S(1)}, f32[2000]{0:T(1024)}, u32[]{:S(2)}) copy-start(f32[2000]{0:T(1024)} %param.8) | copy-start | bytes 24004
  274.2 8.0 %copy-start.1 = (f32[512]{0:T(512)S(1)}, f32[512]{0:T(512)}, u32[]{:S(2)}) copy-start(f32[512]{0:T(512)} %param.9) | copy-start | bytes 6148
Sparse Core Ops, SparseCore 0:
  8.9 31.1 all-gather.3
  41.7 213.3 all-gather.5
  282.2 109.3 all-reduce.1
